TPU v7x, 32 devices: a whole 2x2x4 slice. The times are simulated.
32 devices in a mesh: row: 4 (over x, core), col: 8 (over z, y).
Axes of the slice: x: 2, y: 2, z: 4, core: 2. Of those that a mesh axis runs over, the one named last changes fastest.
Arguments:
- x_rows: float32 [16, 16384], P(None, ('row', 'col')), may hold values from -6 to 6
- alpha_rows: float32 [16384], P(('row', 'col')), may hold values from -0.5 to 1.5
- x_cols: float32 [16, 8192], P(None, ('col', 'row')), may hold values from -6 to 6
- alpha_cols: float32 [8192], P(('col', 'row')), may hold values from -0.0073242188 to 0.021972656
- lengthscale: float32 [16], replicated, may hold values from 1.2 to 2.5
Outputs:
- row_terms: float32 [16, 16384], P(None, ('row', 'col'))
- kernel_alpha: float32 [16384], P(('row', 'col'))
- grad: float32 [16], replicated
All inputs are finite; a program needn't handle non-finite values.
Results may differ from a plain program's by a relative error of at most 0.00021.
Values sent between devices are 32-bit elements; how exact they have to be, the bound alone decides.
A program may use at most 64 MiB of HBM per device.

v0:
```python
import functools

import jax
import jax.numpy as jnp
from jax import lax
from jax.experimental import pallas as pl
from jax.experimental.pallas import tpu as pltpu
from jax.sharding import PartitionSpec as P

LOG2E = 1.4426950408889634
CORES = 2
MESH = pl.DeviceIdType.MESH
F32 = jnp.float32
BF16 = jnp.bfloat16


def split3(value):
    high = value.astype(BF16)
    rest = value - high.astype(F32)
    mid = rest.astype(BF16)
    low = (rest - mid.astype(F32)).astype(BF16)
    return high, mid, low


def stack_rows(count, rows):
    index = lax.broadcasted_iota(jnp.int32, (16, count), 0)
    out = jnp.zeros((16, count), F32)
    for place, row in enumerate(rows):
        row = row.astype(F32) if hasattr(row, "astype") else row
        out = jnp.where(index == place, row, out)
    return out.astype(BF16)


def kernel(
    row_size,
    col_size,
    xr_hbm,
    ar_hbm,
    xc_hbm,
    ac_hbm,
    ls_hbm,
    terms_hbm,
    sums_hbm,
    grad_hbm,
    xr_ref,
    ar_ref,
    ls_ref,
    terms_ref,
    sums_ref,
    grad_ref,
    chunks,
    acc,
    row_aug,
    part,
    parts,
    local,
    send_c,
    recv_c,
    send_f,
    recv_f,
    send_g,
    recv_g,
):
    dims, row_count = xr_ref.shape
    col_count = chunks.shape[2]
    n_x = row_size // CORES
    n_y = n_x if col_size % n_x == 0 else 1
    n_z = col_size // n_y
    n_plane = n_x * n_y
    n = n_x * col_size
    n_all = row_size * col_size
    my_row = lax.axis_index("row")
    my_col = lax.axis_index("col")
    my_z = my_col // n_y
    my_y = my_col % n_y
    partner = (my_row + 1 - 2 * (my_row % CORES), my_col)

    def line_peer(j):
        return (my_row, (my_z + j) % n_z * n_y + my_y)

    def plane_peer(m):
        return (
            (my_row + CORES * (m % n_x)) % row_size,
            my_z * n_y + (my_y + m // n_x) % n_y,
        )

    def any_peer(step):
        d_row = step % row_size
        d_col = step // row_size
        return ((my_row + d_row) % row_size, (my_col + d_col) % col_size)

    def loads():
        return [
            pltpu.make_async_copy(xc_hbm, chunks.at[0, pl.ds(0, dims)], local.at[0]),
            pltpu.make_async_copy(ac_hbm, chunks.at[0, pl.ds(dims, 1)], local.at[1]),
            pltpu.make_async_copy(xr_hbm, xr_ref, local.at[2]),
            pltpu.make_async_copy(ar_hbm, ar_ref, local.at[3]),
            pltpu.make_async_copy(ls_hbm, ls_ref, local.at[4]),
        ]

    for copy in loads():
        copy.start()

    barrier = pltpu.get_barrier_semaphore()

    pl.semaphore_signal(barrier, inc=1, device_id=partner, device_id_type=MESH)

    @pl.loop(1, n_plane)
    def _(m):
        pl.semaphore_signal(barrier, inc=1, device_id=plane_peer(m), device_id_type=MESH)

    @pl.loop(1, n_z)
    def _(j):
        pl.semaphore_signal(barrier, inc=1, device_id=line_peer(j), device_id_type=MESH)

    def line_copy(j):
        return pltpu.make_async_remote_copy(
            chunks.at[0], chunks.at[j], send_c.at[j], recv_c.at[j], line_peer(j), MESH
        )

    def plane_copy(j, m):
        slot = m * n_z + j
        return pltpu.make_async_remote_copy(
            chunks.at[j], chunks.at[slot], send_c.at[slot], recv_c.at[slot], plane_peer(m), MESH
        )

    def forward(slot):
        return pltpu.make_async_remote_copy(
            chunks.at[slot], chunks.at[n + slot], send_f.at[slot], recv_f.at[slot], partner, MESH
        )

    def g_copy(step):
        return pltpu.make_async_remote_copy(
            part.at[pl.ds(0, 1)],
            parts.at[step],
            send_g.at[step],
            recv_g.at[step],
            any_peer(step),
            MESH,
        )

    for copy in loads():
        copy.wait()

    eye = lax.broadcasted_iota(jnp.int32, (dims, dims), 0) == lax.broadcasted_iota(
        jnp.int32, (dims, dims), 1
    )
    scale = jnp.sum(jnp.where(eye, jnp.broadcast_to(ls_ref[...], (dims, dims)), 0.0), 1, keepdims=True)
    inverse = 1.0 / scale
    row_scaled = xr_ref[...] * inverse
    row_norm = (-0.5 * LOG2E) * jnp.sum(row_scaled * row_scaled, 0, keepdims=True)
    rh, rm, rl = split3(row_scaled * LOG2E)
    row_aug[...] = jnp.concatenate(
        [rh, rh, rh, rm, rm, rl, stack_rows(row_count, (1.0, 1.0, 1.0) + split3(row_norm))], 0
    )

    def operands(x, alpha):
        scaled = x * inverse
        norm = (-0.5 * LOG2E) * jnp.sum(scaled * scaled, 0, keepdims=True)
        ch, cm, cl = split3(scaled)
        col_aug = jnp.concatenate(
            [ch, cm, cl, ch, cm, ch, stack_rows(col_count, split3(norm) + (1.0, 1.0, 1.0))], 0
        )
        first = alpha * scaled
        fh, fm, fl = split3(first)
        sh, sm, sl = split3(first * scaled)
        group = stack_rows(col_count, split3(alpha))
        zero = jnp.zeros_like(fl)
        left_high = jnp.concatenate([fh, sh, fm, sm, fl, sl, group], 0)
        left_mid = jnp.concatenate([fh, sh, fm, sm, zero, zero, group], 0)
        exponent = lax.dot_general(
            col_aug, row_aug[...], (((0,), (0,)), ((), ())), preferred_element_type=F32
        )
        value = jnp.exp2(exponent)
        high = value.astype(BF16)
        mid = (value - high.astype(F32)).astype(BF16)
        return [left_high, left_mid], [high, mid]

    def contribute(slots):
        left, right = [], []
        for slot in slots:
            more_left, more_right = operands(
                chunks[slot, 0:dims], chunks[slot, dims : dims + 1]
            )
            left += more_left
            right += more_right
        return jnp.dot(
            jnp.concatenate(left, 1), jnp.concatenate(right, 0), preferred_element_type=F32
        )

    def in_groups(slots):
        slots = list(slots)
        for at in range(0, len(slots), 4):
            acc[...] += contribute(slots[at : at + 4])

    width = 2 if (n - n_z) % 2 == 0 else 1
    acc[...] = contribute([0])

    pl.semaphore_wait(barrier, n_plane + n_z - 1)

    @pl.loop(1, n_z)
    def _(j):
        line_copy(j).start()

    @pl.loop(1, n_plane)
    def _(m):
        plane_copy(0, m).start()

    forward(0).start()

    @pl.loop(1, n_z)
    def _(j):
        line_copy(j).wait_recv()

        @pl.loop(1, n_plane)
        def _(m):
            plane_copy(j, m).start()

        forward(j).start()

    forward(0).wait_recv()
    lag = n_z - 1
    in_groups([n] + list(range(1, n_z)))

    @pl.loop(0, (n - n_z) // width)
    def _(group):
        slots = [n_z + group * width + k for k in range(width)]
        for slot in slots:
            line_copy(slot).wait_recv()
            forward(slot).start()
        for slot in slots:
            forward(slot - lag).wait_recv()
        acc[...] += contribute(slots + [n + slot - lag for slot in slots])

    @pl.loop(n - lag, n)
    def _(slot):
        forward(slot).wait_recv()

    in_groups(range(2 * n - lag, 2 * n))

    total = acc[...]
    first = total[0:16] + total[32:48] + total[64:80]
    second = total[16:32] + total[48:64] + total[80:96]
    weight = total[96:97] + total[97:98] + total[98:99]
    terms = (0.5 * ar_ref[...]) * (
        row_scaled * row_scaled * weight - 2.0 * row_scaled * first + second
    )
    folded = terms[:, 0:128]
    for at in range(128, row_count, 128):
        folded = folded + terms[:, at : at + 128]
    gathered = lax.dot_general(
        jnp.ones((8, 128), F32),
        folded,
        (((1,), (1,)), ((), ())),
        precision=lax.Precision.HIGHEST,
        preferred_element_type=F32,
    )
    part[...] = jnp.zeros_like(part)
    part[:, 0:dims] = gathered
    terms_ref[...] = terms
    sums_ref[...] = weight

    stores = [
        pltpu.make_async_copy(terms_ref, terms_hbm, local.at[0]),
        pltpu.make_async_copy(sums_ref, sums_hbm, local.at[1]),
    ]
    for copy in stores:
        copy.start()

    @pl.loop(1, n_all)
    def _(step):
        g_copy(step).start()

    @pl.loop(1, n)
    def _(slot):
        line_copy(slot).wait_send()

    @pl.loop(0, n)
    def _(slot):
        forward(slot).wait_send()

    for copy in stores:
        copy.wait()
    parts[0] = part[0:1]

    @pl.loop(1, n_all)
    def _(step):
        g_copy(step).wait()

    grad_ref[...] = (jnp.sum(parts[...], 0) / (row_count * n_all))[:, 0:dims]
    copy = pltpu.make_async_copy(grad_ref, grad_hbm, local.at[2])
    copy.start()
    copy.wait()


def settle(terms_in, sums_in, grad_in, terms_out, sums_out, grad_out):
    terms_out[...] = terms_in[...]
    sums_out[...] = sums_in[...]
    grad_out[...] = grad_in[...]


def on_device(row_size, col_size, x_rows, alpha_rows, x_cols, alpha_cols, lengthscale):
    dims, row_count = x_rows.shape
    col_count = x_cols.shape[1]
    n = row_size // CORES * col_size
    n_all = row_size * col_size
    vmem = pl.BlockSpec(memory_space=pltpu.VMEM)
    anywhere = pl.BlockSpec(memory_space=pl.ANY)
    dma = pltpu.SemaphoreType.DMA
    terms, sums, grad = pl.pallas_call(
        functools.partial(kernel, row_size, col_size),
        out_shape=(
            jax.ShapeDtypeStruct((dims, row_count), F32),
            jax.ShapeDtypeStruct((1, row_count), F32),
            jax.ShapeDtypeStruct((1, dims), F32),
        ),
        in_specs=[anywhere] * 5,
        out_specs=(anywhere, anywhere, anywhere),
        scratch_shapes=[
            pltpu.VMEM((dims, row_count), F32),
            pltpu.VMEM((1, row_count), F32),
            pltpu.VMEM((1, dims), F32),
            pltpu.VMEM((dims, row_count), F32),
            pltpu.VMEM((1, row_count), F32),
            pltpu.VMEM((1, dims), F32),
            pltpu.VMEM((2 * n, dims + 1, col_count), F32),
            pltpu.VMEM((112, row_count), F32),
            pltpu.VMEM((112, row_count), BF16),
            pltpu.VMEM((8, 128), F32),
            pltpu.VMEM((n_all, 1, 128), F32),
            dma((5,)),
        ]
        + [dma((n,))] * 4
        + [dma((n_all,))] * 2,
        compiler_params=pltpu.CompilerParams(collective_id=0, has_side_effects=True),
    )(
        x_rows,
        alpha_rows.reshape(1, row_count),
        x_cols,
        alpha_cols.reshape(1, col_count),
        lengthscale.reshape(1, dims),
    )
    terms, sums, grad = pl.pallas_call(
        settle,
        out_shape=(terms, sums, grad),
        in_specs=[vmem] * 3,
        out_specs=(vmem, vmem, vmem),
    )(terms, sums, grad)
    return terms, sums.reshape(row_count), grad.reshape(dims)


def solution(mesh):
    return jax.shard_map(
        functools.partial(on_device, mesh.shape["row"], mesh.shape["col"]),
        mesh=mesh,
        in_specs=(
            P(None, ("row", "col")),
            P(("row", "col")),
            P(None, ("col", "row")),
            P(("col", "row")),
            P(),
        ),
        out_specs=(P(None, ("row", "col")), P(("row", "col")), P()),
        check_vma=False,
    )
```

profile of v0, /device:TPU:0, one launch (start us, length us, event | category | flops | bytes accessed | tf_op | source)
XLA Modules:
  0.0 26.4 jit_solution(62758965822554039)
XLA Ops:
  0.6 24.3 %shard_map.76 = (f32[16,512]{1,0:T(8,128)}, f32[1,512]{1,0:T(1,128)}, f32[1,16]{1,0:T(1,128)}) custom-call(f32[16,512]{1,0:T(8,128)} %xr_hbm.1, f32[1,512]{1,0:T(1,128)} %bitcast.5, f32[16,256]{1,0:T(8,128)} %xc_hbm.1, f32[1,256]{1,0:T(1,128)} %bitcast.6, f32[1,16]{1,0:T(1,128)} %bitcast.7), custom_call_target="tpu_custom_call" | custom-call | tf_op jit(solution)/shard_map/pallas_call | solution.py:310
  25.0 1.4 %shard_map.77 = (f32[16,512]{1,0:T(8,128)}, f32[1,512]{1,0:T(1,128)}, f32[1,16]{1,0:T(1,128)}) custom-call(f32[16,512]{1,0:T(8,128)} %get-tuple-element.9.terms_in, f32[1,512]{1,0:T(1,128)} %get-tuple-element.10.sums_in, f32[1,16]{1,0:T(1,128)} %get-tuple-element.11.grad_in), custom_call_target="tpu_custom_call" | custom-call | tf_op jit(solution)/shard_map/pallas_call | solution.py:343
where the time goes:
time: 26.6 us; the launch traced here: 26.4 us
  Pallas kernels  25.7 us (97%)
  between operations  0.64 us (2%)
    pallas_call x1, Pallas kernels, on_device(): pl.pallas_call(functools.partial(kernel, row_size, col_size), out_shape=(...  24.3 us
    pallas_call x1, Pallas kernels, on_device(): pl.pallas_call(settle, out_shape=(terms, sums, grad), in_specs=[vmem] * 3...  1.39 us

commit v1 on v0

v1 whole, which is shorter than its diff:
```python
import functools

import jax
import jax.numpy as jnp
from jax import lax
from jax.experimental import pallas as pl
from jax.experimental.pallas import tpu as pltpu
from jax.sharding import PartitionSpec as P

LOG2E = 1.4426950408889634
CORES = 2
MESH = pl.DeviceIdType.MESH
F32 = jnp.float32
BF16 = jnp.bfloat16
scope = jax.named_scope


def split3(value):
    high = value.astype(BF16)
    rest = value - high.astype(F32)
    mid = rest.astype(BF16)
    low = (rest - mid.astype(F32)).astype(BF16)
    return high, mid, low


def split2(value):
    high = value.astype(BF16)
    mid = (value - high.astype(F32)).astype(BF16)
    return high, mid


def stack_rows(count, rows):
    index = lax.broadcasted_iota(jnp.int32, (16, count), 0)
    out = jnp.zeros((16, count), F32)
    for place, row in enumerate(rows):
        row = row.astype(F32) if hasattr(row, "astype") else row
        out = jnp.where(index == place, row, out)
    return out.astype(BF16)


def layout(row_size, col_size):
    n_x = row_size // CORES
    n_y = n_x if col_size % n_x == 0 else 1
    return n_x, n_y, col_size // n_y


def far_first(row_size, col_size):
    n_x, n_y, n_z = layout(row_size, col_size)
    steps = [
        (dx, core, dz, dy)
        for dx in range(n_x)
        for core in range(CORES)
        for dz in range(n_z)
        for dy in range(n_y)
    ]
    steps.remove((0, 0, 0, 0))

    def hops(step):
        dx, core, dz, dy = step
        return min(dx, n_x - dx) + min(dy, n_y - dy) + min(dz, n_z - dz), core

    return sorted(steps, key=hops, reverse=True)


def kernel(
    row_size,
    col_size,
    xr_hbm,
    ar_hbm,
    xc_hbm,
    ac_hbm,
    ls_hbm,
    terms_ref,
    sums_ref,
    grad_ref,
    ls_ref,
    rows,
    cols,
    row_aug,
    acc,
    shares,
    incoming,
    part,
    parts,
    local,
    ready,
    send_r,
    recv_r,
    send_y,
    recv_y,
    send_n,
    recv_n,
    send_f,
    recv_f,
    send_t,
    recv_t,
    send_g,
    recv_g,
):
    n_rows, wide, row_count = rows.shape
    dims = wide - 1
    col_count = cols.shape[3]
    n_x, n_y, n_z = layout(row_size, col_size)
    n_all = row_size * col_size
    my_row = lax.axis_index("row")
    my_col = lax.axis_index("col")
    my_x, my_core = my_row // CORES, my_row % CORES
    my_z, my_y = my_col // n_y, my_col % n_y

    def row_peer(k):
        return (
            (my_x + k // CORES) % n_x * CORES + (my_core + k % CORES) % CORES,
            my_col,
        )

    def back(k):
        return (n_x - k // CORES) % n_x * CORES + k % CORES

    def y_peer(m):
        return (my_row, my_z * n_y + (my_y + m) % n_y)

    def z_peer(z):
        return (my_row, z * n_y + my_y)

    above, below = my_z < n_z - 1, my_z > 0
    sides = ((1, above), (-1, below))

    barrier = pltpu.get_barrier_semaphore()
    for sign, there in sides:

        @pl.when(there)
        def _():
            pl.semaphore_signal(
                barrier, inc=1, device_id=z_peer(my_z + sign), device_id_type=MESH
            )

    for m in range(1, n_y):
        pl.semaphore_signal(barrier, inc=1, device_id=y_peer(m), device_id_type=MESH)
    for k in range(row_size - 1, 0, -1):
        pl.semaphore_signal(barrier, inc=1, device_id=row_peer(k), device_id_type=MESH)

    loads = [
        pltpu.make_async_copy(xc_hbm, cols.at[my_z, 0, pl.ds(0, dims)], local.at[0]),
        pltpu.make_async_copy(ac_hbm, cols.at[my_z, 0, pl.ds(dims, 1)], local.at[1]),
        pltpu.make_async_copy(xr_hbm, rows.at[0, pl.ds(0, dims)], local.at[2]),
        pltpu.make_async_copy(ar_hbm, rows.at[0, pl.ds(dims, 1)], local.at[3]),
        pltpu.make_async_copy(ls_hbm, ls_ref, local.at[4]),
    ]
    for copy in loads:
        copy.start()

    def remote(src, dst, send, recv, peer):
        return pltpu.make_async_remote_copy(src, dst, send, recv, peer, MESH)

    def row_copy(k):
        return remote(
            rows.at[0], rows.at[back(k)], send_r.at[k], recv_r.at[back(k)], row_peer(k)
        )

    def row_arrival(k):
        return remote(rows.at[0], rows.at[k], send_r.at[k], recv_r.at[k], row_peer(k))

    def y_copy(m):
        at = n_y - m
        return remote(
            cols.at[my_z, 0], cols.at[my_z, at], send_y.at[m], recv_y.at[at], y_peer(m)
        )

    def y_arrival(m):
        return remote(
            cols.at[my_z, 0], cols.at[my_z, m], send_y.at[m], recv_y.at[m], y_peer(m)
        )

    def near_copy(sign, m):
        return remote(
            cols.at[my_z, m],
            cols.at[my_z, m],
            send_n.at[(sign + 1) // 2, m],
            recv_n.at[my_z, m],
            z_peer(my_z + sign),
        )

    def near_arrival(z, m):
        return remote(
            cols.at[z, m], cols.at[z, m], send_n.at[0, m], recv_n.at[z, m], z_peer(z)
        )

    def far_copy(z):
        return remote(cols.at[my_z], cols.at[my_z], send_f.at[z], recv_f.at[my_z], z_peer(z))

    def far_arrival(z):
        return remote(cols.at[z], cols.at[z], send_f.at[z], recv_f.at[z], z_peer(z))

    def term_copy(k):
        return remote(
            shares.at[k], incoming.at[back(k)], send_t.at[k], recv_t.at[back(k)], row_peer(k)
        )

    def term_arrival(k):
        return remote(shares.at[k], incoming.at[k], send_t.at[k], recv_t.at[k], row_peer(k))

    steps = far_first(row_size, col_size)

    def g_copy(place):
        dx, core, dz, dy = steps[place]
        peer = (
            (my_x + dx) % n_x * CORES + (my_core + core) % CORES,
            (my_z + dz) % n_z * n_y + (my_y + dy) % n_y,
        )
        return remote(
            part.at[pl.ds(0, 1)], parts.at[place], send_g.at[place], recv_g.at[place], peer
        )

    with scope("load"):
        for copy in loads:
            copy.wait()

    eye = lax.broadcasted_iota(jnp.int32, (dims, dims), 0) == lax.broadcasted_iota(
        jnp.int32, (dims, dims), 1
    )
    scale = jnp.sum(jnp.where(eye, jnp.broadcast_to(ls_ref[...], (dims, dims)), 0.0), 1, keepdims=True)
    inverse = 1.0 / scale

    def prepare_rows(k):
        row_scaled = rows[k, 0:dims] * inverse
        row_norm = (-0.5 * LOG2E) * jnp.sum(row_scaled * row_scaled, 0, keepdims=True)
        rh, rm, rl = split3(row_scaled * LOG2E)
        row_aug[k] = jnp.concatenate(
            [rh, rh, rh, rm, rm, rl, stack_rows(row_count, (1.0, 1.0, 1.0) + split3(row_norm))], 0
        )

    def operands(z, m):
        x, alpha = cols[z, m, 0:dims], cols[z, m, dims : dims + 1]
        scaled = x * inverse
        norm = (-0.5 * LOG2E) * jnp.sum(scaled * scaled, 0, keepdims=True)
        ch, cm, cl = split3(scaled)
        col_aug = jnp.concatenate(
            [ch, cm, cl, ch, cm, ch, stack_rows(col_count, split3(norm) + (1.0, 1.0, 1.0))], 0
        )
        first = alpha * scaled
        fh, fm = split2(first)
        sh, sm = split2(first * scaled)
        left = jnp.concatenate([fh, sh, fm, sm, stack_rows(col_count, split3(alpha))], 0)
        return col_aug, left

    def contribute(chunks, blocks, fresh=False):
        made = [operands(z, m) for z, m in chunks]
        steps = [(k, at) for k in blocks for at in range(len(chunks))]
        exponents, values = {}, {}
        for now in range(len(steps) + 2):
            if now < len(steps):
                k, at = steps[now]
                exponents[now] = lax.dot_general(
                    made[at][0], row_aug[k], (((0,), (0,)), ((), ())), preferred_element_type=F32
                )
            if now >= 2:
                k, at = steps[now - 2]
                left = made[at][1]
                more = jnp.dot(
                    jnp.concatenate([left, left], 1),
                    jnp.concatenate(values.pop(now - 2), 0),
                    preferred_element_type=F32,
                )
                if fresh and at == 0:
                    acc[k] = more
                else:
                    acc[k] += more
            if 1 <= now <= len(steps):
                values[now - 1] = split2(jnp.exp2(exponents.pop(now - 1)))

    prepare_rows(0)

    with scope("bar"):
        pl.semaphore_wait(barrier, row_size + n_y - 2 + sum(there.astype(jnp.int32) for _, there in sides))

    with scope("near"):
        @pl.when(jnp.logical_and(above, below))
        def _():
            for sign in (1, -1):
                pl.semaphore_signal(
                    ready.at[my_z + sign],
                    inc=1,
                    device_id=z_peer(my_z - sign),
                    device_id_type=MESH,
                )

        for m in range(1, n_y):
            y_copy(m).start()
        for sign, there in sides:

            @pl.when(there)
            def _():
                near_copy(sign, 0).start()

        for k in list(range(CORES, row_size)) + [1]:
            row_copy(k).start()

    with scope("c00"):
        contribute([(my_z, 0)], [0], fresh=True)

    def learn(d):
        for sign, there in sides:
            opposite = my_z - sign
            z = my_z + sign * d
            inside = jnp.logical_and(z >= 0, z < n_z)

            @pl.when(inside)
            def _():
                pl.semaphore_wait(ready.at[z], 1)

            @pl.when(jnp.logical_and(inside, jnp.logical_and(opposite >= 0, opposite < n_z)))
            def _():
                pl.semaphore_signal(
                    ready.at[z], inc=1, device_id=z_peer(opposite), device_id_type=MESH
                )

    def send_far(d):
        for sign, _ in sides:
            z = my_z + sign * d

            @pl.when(jnp.logical_and(z >= 0, z < n_z))
            def _():
                far_copy(z).start()

    if n_z > 2:
        with scope("rdy2"):
            learn(2)

    with scope("c01"):
        row_arrival(1).wait_recv()
        prepare_rows(1)
        contribute([(my_z, 0)], [1], fresh=True)

    with scope("ywait"):
        for m in range(1, n_y):
            y_arrival(m).wait_recv()

    with scope("fsend"):
        if n_z > 2:
            send_far(2)
        for sign, there in sides:

            @pl.when(there)
            def _():
                for m in range(1, n_y):
                    near_copy(sign, m).start()

    with scope("cy"):
        contribute([(my_z, m) for m in range(1, n_y)], [0, 1])

    with scope("rdy3"):
        for d in range(3, n_z):
            learn(d)
            send_far(d)

    with scope("roww"):
        for k in range(CORES, row_size):
            row_arrival(k).wait_recv()
    with scope("crow"):
        for k in range(CORES, row_size):
            prepare_rows(k)
        contribute([(my_z, m) for m in range(n_y)], range(CORES, row_size), fresh=True)

    low = jnp.minimum(my_z, n_z - 1 - my_z)
    far_sign = jnp.where(2 * my_z < n_z - 1, 1, -1)
    for t in range(1, n_z):
        near_z = my_z + (1 if t % 2 else -1) * ((t + 1) // 2)
        z = jnp.where(t <= 2 * low, near_z, my_z + far_sign * (t - low))
        is_near = jnp.logical_or(z == my_z + 1, z == my_z - 1)
        with scope("zw"):

            @pl.when(is_near)
            def _():
                for m in range(n_y):
                    near_arrival(z, m).wait_recv()

            @pl.when(jnp.logical_not(is_near))
            def _():
                far_arrival(z).wait_recv()

        with scope("cz"):
            contribute([(z, m) for m in range(n_y)], range(row_size))

    with scope("fold"):
        folded = None
        for k in range(row_size):
            total = acc[k]
            row_scaled = rows[k, 0:dims] * inverse
            first = total[0:16] + total[32:48]
            second = total[16:32] + total[48:64]
            weight = total[64:65] + total[65:66] + total[66:67]
            share = (0.5 * rows[k, dims : dims + 1]) * (
                row_scaled * row_scaled * weight - 2.0 * row_scaled * first + second
            )
            shares[k, 0:dims] = share
            shares[k, dims : dims + 1] = weight
            for at in range(0, row_count, 128):
                piece = share[:, at : at + 128]
                folded = piece if folded is None else folded + piece
        gathered = lax.dot_general(
            jnp.ones((8, 128), F32),
            folded,
            (((1,), (1,)), ((), ())),
            precision=lax.Precision.HIGHEST,
            preferred_element_type=F32,
        )
        part[...] = jnp.zeros_like(part)
        part[:, 0:dims] = gathered

    with scope("gst"):
        for place in range(n_all - 1):
            g_copy(place).start()
        for k in list(range(CORES, row_size)) + [1]:
            term_copy(k).start()

    with scope("drain"):
        for m in range(1, n_y):
            y_copy(m).wait_send()
        for k in range(1, row_size):
            row_copy(k).wait_send()
        for sign, there in sides:

            @pl.when(there)
            def _():
                for m in range(n_y):
                    near_copy(sign, m).wait_send()

            for d in range(2, n_z):
                z = my_z + sign * d

                @pl.when(jnp.logical_and(z >= 0, z < n_z))
                def _():
                    far_copy(z).wait_send()

    with scope("twait"):
        for k in range(1, row_size):
            term_arrival(k).wait_recv()
    with scope("tsum"):
        whole = shares[0]
        for k in range(1, row_size):
            whole = whole + incoming[k]
        terms_ref[...] = whole[0:dims]
        sums_ref[...] = whole[dims : dims + 1]
        parts[n_all - 1] = part[0:1]
    with scope("gwait"):
        for place in range(n_all - 1):
            g_copy(place).wait()
    with scope("gsum"):
        grad_ref[...] = (jnp.sum(parts[...], 0) / (row_count * n_all))[:, 0:dims]
        for k in range(1, row_size):
            term_copy(k).wait_send()


def settle(terms_in, sums_in, grad_in, terms_out, sums_out, grad_out, sems):
    copies = [
        pltpu.make_async_copy(terms_in, terms_out, sems.at[0]),
        pltpu.make_async_copy(sums_in, sums_out, sems.at[1]),
        pltpu.make_async_copy(grad_in, grad_out, sems.at[2]),
    ]
    for copy in copies:
        copy.start()
    for copy in copies:
        copy.wait()


def on_device(row_size, col_size, x_rows, alpha_rows, x_cols, alpha_cols, lengthscale):
    dims, row_count = x_rows.shape
    col_count = x_cols.shape[1]
    _, n_y, n_z = layout(row_size, col_size)
    n_all = row_size * col_size
    vmem = pl.BlockSpec(memory_space=pltpu.VMEM)
    anywhere = pl.BlockSpec(memory_space=pl.ANY)
    dma = pltpu.SemaphoreType.DMA
    terms, sums, grad = pl.pallas_call(
        functools.partial(kernel, row_size, col_size),
        out_shape=(
            pltpu.VMEM((dims, row_count), F32),
            pltpu.VMEM((1, row_count), F32),
            pltpu.VMEM((1, dims), F32),
        ),
        in_specs=[pl.BlockSpec(memory_space=pltpu.HBM)] * 5,
        out_specs=(vmem, vmem, vmem),
        scratch_shapes=[
            pltpu.VMEM((1, dims), F32),
            pltpu.VMEM((row_size, dims + 1, row_count), F32),
            pltpu.VMEM((n_z, n_y, dims + 1, col_count), F32),
            pltpu.VMEM((row_size, 112, row_count), BF16),
            pltpu.VMEM((row_size, 80, row_count), F32),
            pltpu.VMEM((row_size, dims + 1, row_count), F32),
            pltpu.VMEM((row_size, dims + 1, row_count), F32),
            pltpu.VMEM((8, 128), F32),
            pltpu.VMEM((n_all, 1, 128), F32),
            dma((5,)),
            pltpu.SemaphoreType.REGULAR((n_z,)),
            dma((row_size,)),
            dma((row_size,)),
            dma((n_y,)),
            dma((n_y,)),
            dma((2, n_y)),
            dma((n_z, n_y)),
            dma((n_z,)),
            dma((n_z,)),
            dma((row_size,)),
            dma((row_size,)),
            dma((n_all,)),
            dma((n_all,)),
        ],
        compiler_params=pltpu.CompilerParams(
            collective_id=0, has_side_effects=True
        ),
    )(
        x_rows,
        alpha_rows.reshape(1, row_count),
        x_cols,
        alpha_cols.reshape(1, col_count),
        lengthscale.reshape(1, dims),
    )
    terms, sums, grad = pl.pallas_call(
        settle,
        out_shape=[jax.ShapeDtypeStruct(x.shape, x.dtype) for x in (terms, sums, grad)],
        in_specs=[vmem] * 3,
        out_specs=(anywhere, anywhere, anywhere),
        scratch_shapes=[dma((3,))],
        compiler_params=pltpu.CompilerParams(vmem_limit_bytes=16 * 1024 * 1024),
    )(terms, sums, grad)
    return terms, sums.reshape(row_count), grad.reshape(dims)


def solution(mesh):
    return jax.shard_map(
        functools.partial(on_device, mesh.shape["row"], mesh.shape["col"]),
        mesh=mesh,
        in_specs=(
            P(None, ("row", "col")),
            P(("row", "col")),
            P(None, ("col", "row")),
            P(("col", "row")),
            P(),
        ),
        out_specs=(P(None, ("row", "col")), P(("row", "col")), P()),
        check_vma=False,
    )
```

time: 26.6 us -> 22.3 us (0.84)
  Pallas kernels: 25.7 us -> 21.4 us
    pallas_call x1, Pallas kernels: 24.3 us -> 20.8 us  [on_device(): pl.pallas_call(functools.partial(kernel, row_size, col_size), out_shape=(...]
    pallas_call x1, Pallas kernels: 1.39 us -> 0.65 us  [on_device(): pl.pallas_call(settle, out_shape=[jax.ShapeDtypeStruct(x.shape, x.dtype)...]
where the time goes in v1:
time: 22.3 us; the launch traced here: 22 us
  Pallas kernels  21.4 us (96%)
  between operations  0.64 us (3%)
    pallas_call x1, Pallas kernels, on_device(): pl.pallas_call(functools.partial(kernel, row_size, col_size), out_shape=(...  20.8 us
    pallas_call x1, Pallas kernels, on_device(): pl.pallas_call(settle, out_shape=[jax.ShapeDtypeStruct(x.shape, x.dtype)...  0.65 us

profile of v1, /device:TPU:0, one launch (start us, length us, event | category | flops | bytes accessed | tf_op | source)
XLA Modules:
  0.0 22.0 jit_solution(2646454503655821507)
XLA Ops:
  0.6 20.8 %shard_map.76 = (f32[16,512]{1,0:T(8,128)S(1)}, f32[1,512]{1,0:T(1,128)S(1)}, f32[1,16]{1,0:T(1,128)S(1)}) custom-call(f32[16,512]{1,0:T(8,128)} %xr_hbm.1, f32[1,512]{1,0:T(1,128)} %bitcast.5, f32[16,256]{1,0:T(8,128)} %xc_hbm.1, f32[1,256]{1,0:T(1,128)} %bitcast.6, f32[1,16]{1,0:T(1,128)} %bitcast.7), custom_call_target="tpu_custom_call" | custom-call | tf_op jit(solution)/shard_map/pallas_call | solution.py:474
  21.4 0.6 %shard_map.77 = (f32[16,512]{1,0:T(8,128)}, f32[1,512]{1,0:T(1,128)}, f32[1,16]{1,0:T(1,128)}) custom-call(f32[16,512]{1,0:T(8,128)S(1)} %get-tuple-element.9.terms_in, f32[1,512]{1,0:T(1,128)S(1)} %get-tuple-element.10.sums_in, f32[1,16]{1,0:T(1,128)S(1)} %get-tuple-element.11.grad_in), custom_call_target="tpu_custom_call" | custom-call | tf_op jit(solution)/shard_map/pallas_call | solution.py:518

commit v2 on v1

v2 whole, which is shorter than its diff:
```python
import functools

import jax
import jax.numpy as jnp
from jax import lax
from jax.experimental import pallas as pl
from jax.experimental.pallas import tpu as pltpu
from jax.sharding import PartitionSpec as P

LOG2E = 1.4426950408889634
CORES = 2
MESH = pl.DeviceIdType.MESH
F32 = jnp.float32
BF16 = jnp.bfloat16
scope = jax.named_scope
LAG = 2


def split3(value):
    high = value.astype(BF16)
    rest = value - high.astype(F32)
    mid = rest.astype(BF16)
    low = (rest - mid.astype(F32)).astype(BF16)
    return high, mid, low


def split2(value):
    high = value.astype(BF16)
    mid = (value - high.astype(F32)).astype(BF16)
    return high, mid


def stack_rows(count, rows):
    index = lax.broadcasted_iota(jnp.int32, (16, count), 0)
    out = jnp.zeros((16, count), F32)
    for place, row in enumerate(rows):
        row = row.astype(F32) if hasattr(row, "astype") else row
        out = jnp.where(index == place, row, out)
    return out.astype(BF16)


def layout(row_size, col_size):
    n_x = row_size // CORES
    n_y = n_x if col_size % n_x == 0 else 1
    return n_x, n_y, col_size // n_y


def far_first(row_size, col_size):
    n_x, n_y, n_z = layout(row_size, col_size)
    steps = [
        (dx, core, dz, dy)
        for dx in range(n_x)
        for core in range(CORES)
        for dz in range(n_z)
        for dy in range(n_y)
    ]
    steps.remove((0, 0, 0, 0))

    def hops(step):
        dx, core, dz, dy = step
        return min(dx, n_x - dx) + min(dy, n_y - dy) + min(dz, n_z - dz), core

    return sorted(steps, key=hops, reverse=True)


def kernel(
    row_size,
    col_size,
    xr_hbm,
    ar_hbm,
    xc_hbm,
    ac_hbm,
    ls_hbm,
    terms_ref,
    sums_ref,
    grad_ref,
    ls_ref,
    rows,
    row_alpha,
    cols,
    col_alpha,
    row_aug,
    acc,
    values,
    lefts,
    shares,
    share_sums,
    incoming,
    incoming_sums,
    part,
    parts,
    local,
    sent,
    recv_r,
    recv_ra,
    recv_c,
    recv_t,
    recv_g,
):
    _, dims, row_count = rows.shape
    col_count = cols.shape[2]
    n_x, n_y, n_z = layout(row_size, col_size)
    n_all = row_size * col_size
    my_row = lax.axis_index("row")
    my_col = lax.axis_index("col")
    my_x, my_core = my_row // CORES, my_row % CORES
    my_z, my_y = my_col // n_y, my_col % n_y

    def row_peer(k):
        return (
            (my_x + k // CORES) % n_x * CORES + (my_core + k % CORES) % CORES,
            my_col,
        )

    def back(k):
        return (n_x - k // CORES) % n_x * CORES + k % CORES

    low = jnp.minimum(my_z, n_z - 1 - my_z)
    far_sign = jnp.where(2 * my_z < n_z - 1, 1, -1)
    order = [my_z]
    for t in range(1, n_z):
        near = my_z + (1 if t % 2 else -1) * ((t + 1) // 2)
        order.append(jnp.where(t <= 2 * low, near, my_z + far_sign * (t - low)))
    places = [
        [z * n_y + (my_y + m) % n_y for m in range(n_y)] for z in order
    ]
    ordered = [c for line in places for c in line]
    col_peers = ordered[1:]
    row_steps = list(range(CORES, row_size)) + [1]

    barrier = pltpu.get_barrier_semaphore()
    for c in reversed(col_peers):
        pl.semaphore_signal(barrier, inc=1, device_id=(my_row, c), device_id_type=MESH)
    for k in row_steps:
        pl.semaphore_signal(barrier, inc=1, device_id=row_peer(k), device_id_type=MESH)

    loads = [
        pltpu.make_async_copy(xc_hbm, cols.at[my_col], local.at[0]),
        pltpu.make_async_copy(ac_hbm, col_alpha.at[my_col], local.at[1]),
        pltpu.make_async_copy(xr_hbm, rows.at[0], local.at[2]),
        pltpu.make_async_copy(ar_hbm, row_alpha.at[0], local.at[3]),
        pltpu.make_async_copy(ls_hbm, ls_ref, local.at[4]),
    ]
    for copy in loads:
        copy.start()

    def remote(src, dst, send, recv, peer):
        return pltpu.make_async_remote_copy(src, dst, send, recv, peer, MESH)

    def row_copy(k, which):
        ref, there = (rows, row_alpha)[which], back(k)
        return remote(
            ref.at[0],
            ref.at[there],
            sent.at[which],
            recv_ra.at[0] if which else recv_r.at[there],
            row_peer(k),
        )

    def bytes_of(ref, count, send, recv):
        return remote(ref.at[pl.ds(0, count)], ref.at[pl.ds(0, count)], send, recv, row_peer(1))

    def row_arrival(k):
        return remote(rows.at[0], rows.at[k], sent.at[0], recv_r.at[k], row_peer(k))

    def col_copy(c, which):
        ref = (cols, col_alpha)[which]
        return remote(
            ref.at[my_col], ref.at[my_col], sent.at[2 + which], recv_c.at[which, my_z], (my_row, c)
        )

    def term_copy(k, which):
        src, dst = ((shares, incoming), (share_sums, incoming_sums))[which]
        there = back(k)
        return remote(
            src.at[k], dst.at[there], sent.at[4 + which], recv_t.at[which], row_peer(k)
        )

    steps = far_first(row_size, col_size)

    def g_copy(place):
        dx, core, dz, dy = steps[place]
        peer = (
            (my_x + dx) % n_x * CORES + (my_core + core) % CORES,
            (my_z + dz) % n_z * n_y + (my_y + dy) % n_y,
        )
        return remote(
            part.at[pl.ds(0, 1)], parts.at[place], sent.at[6], recv_g.at[0], peer
        )

    with scope("load"):
        for copy in loads:
            copy.wait()

    eye = lax.broadcasted_iota(jnp.int32, (dims, dims), 0) == lax.broadcasted_iota(
        jnp.int32, (dims, dims), 1
    )
    scale = jnp.sum(jnp.where(eye, jnp.broadcast_to(ls_ref[...], (dims, dims)), 0.0), 1, keepdims=True)
    inverse = 1.0 / scale

    def prepare_rows(k):
        row_scaled = rows[k] * inverse
        row_norm = (-0.5 * LOG2E) * jnp.sum(row_scaled * row_scaled, 0, keepdims=True)
        rh, rm, rl = split3(row_scaled * LOG2E)
        row_aug[k] = jnp.concatenate(
            [rh, rh, rh, rm, rm, rl, stack_rows(row_count, (1.0, 1.0, 1.0) + split3(row_norm))], 0
        )

    def operands(c):
        x, alpha = cols[c], col_alpha[c]
        scaled = x * inverse
        norm = (-0.5 * LOG2E) * jnp.sum(scaled * scaled, 0, keepdims=True)
        ch, cm, cl = split3(scaled)
        col_aug = jnp.concatenate(
            [ch, cm, cl, ch, cm, ch, stack_rows(col_count, split3(norm) + (1.0, 1.0, 1.0))], 0
        )
        first = alpha * scaled
        fh, fm = split2(first)
        sh, sm = split2(first * scaled)
        group = stack_rows(col_count, split3(alpha))
        left = jnp.concatenate([fh, sh, fm, sm, group] + [jnp.zeros_like(group)] * 3, 0)
        return col_aug, left

    waiting, begun, made = [], set(), {}
    slots = values.shape[0]
    count = 0

    def add_up():
        k, place, slot = waiting.pop(0)
        left = lefts[place]
        more = jnp.dot(
            jnp.concatenate([left, left], 1), values[slot], preferred_element_type=F32
        )
        more = more[0:80]
        if k in begun:
            acc[k] += more
        else:
            acc[k] = more
        begun.add(k)

    def contribute(pairs, last=False):
        nonlocal count
        pairs = list(pairs)
        while waiting:
            add_up()
        augs, exponents = {}, {}

        def settle_values(now):
            nonlocal count
            high, mid = split2(jnp.exp2(exponents.pop(now)))
            slot = count % slots
            count += 1
            values[slot, 0:col_count] = high
            values[slot, col_count : 2 * col_count] = mid
            waiting.append((pairs[now][1], pairs[now][0], slot))

        for now, (place, k) in enumerate(pairs):
            if place not in augs:
                augs[place], left = operands(ordered[place])
                if place not in made:
                    lefts[place] = left
                    made[place] = True
            exponents[now] = lax.dot_general(
                augs[place], row_aug[k], (((0,), (0,)), ((), ())), preferred_element_type=F32
            )
            if len(waiting) >= LAG - 1:
                add_up()
            if now:
                settle_values(now - 1)
        while waiting:
            add_up()
        settle_values(len(pairs) - 1)
        while last and waiting:
            add_up()

    prepare_rows(0)

    with scope("bar"):
        pl.semaphore_wait(barrier, row_size + col_size - 2)

    with scope("send"):
        for k in row_steps:
            row_copy(k, 0).start()
        for c in col_peers:
            col_copy(c, 0).start()
            col_copy(c, 1).start()
        for k in row_steps:
            row_copy(k, 1).start()

    with scope("c00"):
        contribute([(0, 0)], last=True)

    with scope("w01"):
        row_arrival(1).wait_recv()
    with scope("c01"):
        prepare_rows(1)
        contribute([(0, 1)], last=True)

    def arrive(z, chunks):
        for which, ref in enumerate((cols, col_alpha)):
            bytes_of(ref, chunks, sent.at[2 + which], recv_c.at[which, z]).wait_recv()

    with scope("wrow"):
        for k in range(CORES, row_size):
            row_arrival(k).wait_recv()
        if n_y > 1:
            arrive(my_z, n_y - 1)
    with scope("crow"):
        for k in range(CORES, row_size):
            prepare_rows(k)
        contribute(
            [(0, k) for k in range(CORES, row_size)]
            + [(m, k) for m in range(1, n_y) for k in range(row_size)]
        )

    for at in range(1, n_z):
        with scope("wz"):
            arrive(order[at], n_y)
        with scope("cz"):
            contribute(
                [(at * n_y + m, k) for m in range(n_y) for k in range(row_size)],
                last=at == n_z - 1,
            )

    with scope("fold"):
        bytes_of(row_alpha, row_size - 1, sent.at[1], recv_ra.at[0]).wait_recv()
        folded = None
        for k in range(row_size):
            total = acc[k]
            row_scaled = rows[k] * inverse
            first = total[0:16] + total[32:48]
            second = total[16:32] + total[48:64]
            weight = total[64:65] + total[65:66] + total[66:67]
            share = (0.5 * row_alpha[k]) * (
                row_scaled * row_scaled * weight - 2.0 * row_scaled * first + second
            )
            shares[k] = share
            share_sums[k] = weight
            for at in range(0, row_count, 128):
                piece = share[:, at : at + 128]
                folded = piece if folded is None else folded + piece
        gathered = lax.dot_general(
            jnp.ones((8, 128), F32),
            folded,
            (((1,), (1,)), ((), ())),
            precision=lax.Precision.HIGHEST,
            preferred_element_type=F32,
        )
        part[...] = jnp.zeros_like(part)
        part[:, 0:dims] = gathered

    with scope("gst"):
        for place in range(n_all - 1):
            g_copy(place).start()
        for k in row_steps:
            for which in (0, 1):
                term_copy(k, which).start()

    with scope("drain"):
        for which, ref in enumerate((rows, row_alpha)):
            bytes_of(ref, row_size - 1, sent.at[which], recv_r.at[0]).wait_send()
        for which, ref in enumerate((cols, col_alpha)):
            bytes_of(ref, col_size - 1, sent.at[2 + which], recv_r.at[0]).wait_send()

    with scope("twait"):
        for which, ref in enumerate((incoming, incoming_sums)):
            bytes_of(ref, row_size - 1, sent.at[4 + which], recv_t.at[which]).wait_recv()
    with scope("tsum"):
        terms, sums = shares[0], share_sums[0]
        for k in range(1, row_size):
            terms = terms + incoming[k]
            sums = sums + incoming_sums[k]
        terms_ref[...] = terms
        sums_ref[...] = sums
        parts[n_all - 1] = part[0:1]
    with scope("gwait"):
        bytes_of(parts, n_all - 1, sent.at[6], recv_g.at[0]).wait()
    with scope("gsum"):
        grad_ref[...] = (jnp.sum(parts[...], 0) / (row_count * n_all))[:, 0:dims]
        for which, ref in enumerate((shares, share_sums)):
            bytes_of(ref, row_size - 1, sent.at[4 + which], recv_t.at[which]).wait_send()


def settle(terms_in, sums_in, grad_in, terms_out, sums_out, grad_out, sems):
    copies = [
        pltpu.make_async_copy(terms_in, terms_out, sems.at[0]),
        pltpu.make_async_copy(sums_in, sums_out, sems.at[1]),
        pltpu.make_async_copy(grad_in, grad_out, sems.at[2]),
    ]
    for copy in copies:
        copy.start()
    for copy in copies:
        copy.wait()


def on_device(row_size, col_size, x_rows, alpha_rows, x_cols, alpha_cols, lengthscale):
    dims, row_count = x_rows.shape
    col_count = x_cols.shape[1]
    _, _, n_z = layout(row_size, col_size)
    n_all = row_size * col_size
    vmem = pl.BlockSpec(memory_space=pltpu.VMEM)
    anywhere = pl.BlockSpec(memory_space=pl.ANY)
    dma = pltpu.SemaphoreType.DMA
    terms, sums, grad = pl.pallas_call(
        functools.partial(kernel, row_size, col_size),
        out_shape=(
            pltpu.VMEM((dims, row_count), F32),
            pltpu.VMEM((1, row_count), F32),
            pltpu.VMEM((1, dims), F32),
        ),
        in_specs=[pl.BlockSpec(memory_space=pltpu.HBM)] * 5,
        out_specs=(vmem, vmem, vmem),
        scratch_shapes=[
            pltpu.VMEM((1, dims), F32),
            pltpu.VMEM((row_size, dims, row_count), F32),
            pltpu.VMEM((row_size, 1, row_count), F32),
            pltpu.VMEM((col_size, dims, col_count), F32),
            pltpu.VMEM((col_size, 1, col_count), F32),
            pltpu.VMEM((row_size, 112, row_count), BF16),
            pltpu.VMEM((row_size, 80, row_count), F32),
            pltpu.VMEM((LAG + 1, 2 * col_count, row_count), BF16),
            pltpu.VMEM((col_size, 128, col_count), BF16),
            pltpu.VMEM((row_size, dims, row_count), F32),
            pltpu.VMEM((row_size, 1, row_count), F32),
            pltpu.VMEM((row_size, dims, row_count), F32),
            pltpu.VMEM((row_size, 1, row_count), F32),
            pltpu.VMEM((8, 128), F32),
            pltpu.VMEM((n_all, 1, 128), F32),
            dma((5,)),
            dma((7,)),
            dma((row_size,)),
            dma((1,)),
            dma((2, n_z)),
            dma((2,)),
            dma((1,)),
        ],
        compiler_params=pltpu.CompilerParams(
            collective_id=0, has_side_effects=True
        ),
    )(
        x_rows,
        alpha_rows.reshape(1, row_count),
        x_cols,
        alpha_cols.reshape(1, col_count),
        lengthscale.reshape(1, dims),
    )
    terms, sums, grad = pl.pallas_call(
        settle,
        out_shape=[jax.ShapeDtypeStruct(x.shape, x.dtype) for x in (terms, sums, grad)],
        in_specs=[vmem] * 3,
        out_specs=(anywhere, anywhere, anywhere),
        scratch_shapes=[dma((3,))],
        compiler_params=pltpu.CompilerParams(vmem_limit_bytes=16 * 1024 * 1024),
    )(terms, sums, grad)
    return terms, sums.reshape(row_count), grad.reshape(dims)


def solution(mesh):
    return jax.shard_map(
        functools.partial(on_device, mesh.shape["row"], mesh.shape["col"]),
        mesh=mesh,
        in_specs=(
            P(None, ("row", "col")),
            P(("row", "col")),
            P(None, ("col", "row")),
            P(("col", "row")),
            P(),
        ),
        out_specs=(P(None, ("row", "col")), P(("row", "col")), P()),
        check_vma=False,
    )
```

time: 22.3 us -> 20.9 us (0.937)
  Pallas kernels: 21.4 us -> 20 us
    pallas_call x1, Pallas kernels: 20.8 us -> 19.4 us  [on_device(): pl.pallas_call(functools.partial(kernel, row_size, col_size), out_shape=(...]
where the time goes in v2:
time: 20.9 us; the launch traced here: 20.7 us
  Pallas kernels  20 us (96%)
  between operations  0.64 us (3%)
    pallas_call x1, Pallas kernels, on_device(): pl.pallas_call(functools.partial(kernel, row_size, col_size), out_shape=(...  19.4 us
    pallas_call x1, Pallas kernels, on_device(): pl.pallas_call(settle, out_shape=[jax.ShapeDtypeStruct(x.shape, x.dtype)...  0.65 us

profile of v2, /device:TPU:0, one launch (start us, length us, event | category | flops | bytes accessed | tf_op | source)
XLA Modules:
  0.0 20.7 jit_solution(17392077407084007138)
XLA Ops:
  0.6 19.4 %shard_map.76 = (f32[16,512]{1,0:T(8,128)S(1)}, f32[1,512]{1,0:T(1,128)S(1)}, f32[1,16]{1,0:T(1,128)S(1)}) custom-call(f32[16,512]{1,0:T(8,128)} %xr_hbm.1, f32[1,512]{1,0:T(1,128)} %bitcast.5, f32[16,256]{1,0:T(8,128)} %xc_hbm.1, f32[1,256]{1,0:T(1,128)} %bitcast.6, f32[1,16]{1,0:T(1,128)} %bitcast.7), custom_call_target="tpu_custom_call" | custom-call | tf_op jit(solution)/shard_map/pallas_call | solution.py:404
  20.0 0.6 %shard_map.77 = (f32[16,512]{1,0:T(8,128)}, f32[1,512]{1,0:T(1,128)}, f32[1,16]{1,0:T(1,128)}) custom-call(f32[16,512]{1,0:T(8,128)S(1)} %get-tuple-element.9.terms_in, f32[1,512]{1,0:T(1,128)S(1)} %get-tuple-element.10.sums_in, f32[1,16]{1,0:T(1,128)S(1)} %get-tuple-element.11.grad_in), custom_call_target="tpu_custom_call" | custom-call | tf_op jit(solution)/shard_map/pallas_call | solution.py:447

commit v3 on v2

--- a/solution.py
+++ b/solution.py
@@ -90,6 +90,7 @@
     part,
     parts,
     local,
+    ready,
     sent,
     recv_r,
     recv_ra,
@@ -125,12 +126,22 @@
         [z * n_y + (my_y + m) % n_y for m in range(n_y)] for z in order
     ]
     ordered = [c for line in places for c in line]
-    col_peers = ordered[1:]
     row_steps = list(range(CORES, row_size)) + [1]
+    sides = [(1, my_z < n_z - 1), (-1, my_z > 0)]
+
+    def line(z):
+        return [(my_row, z * n_y + (my_y + m) % n_y) for m in range(n_y)]
 
     barrier = pltpu.get_barrier_semaphore()
-    for c in reversed(col_peers):
-        pl.semaphore_signal(barrier, inc=1, device_id=(my_row, c), device_id_type=MESH)
+    for sign, there in sides:
+
+        @pl.when(there)
+        def _():
+            for peer in reversed(line(my_z + sign)):
+                pl.semaphore_signal(barrier, inc=1, device_id=peer, device_id_type=MESH)
+
+    for peer in line(my_z)[1:]:
+        pl.semaphore_signal(barrier, inc=1, device_id=peer, device_id_type=MESH)
     for k in row_steps:
         pl.semaphore_signal(barrier, inc=1, device_id=row_peer(k), device_id_type=MESH)
 
@@ -163,11 +174,39 @@
     def row_arrival(k):
         return remote(rows.at[0], rows.at[k], sent.at[0], recv_r.at[k], row_peer(k))
 
-    def col_copy(c, which):
+    def col_copy(peer, which, across):
         ref = (cols, col_alpha)[which]
         return remote(
-            ref.at[my_col], ref.at[my_col], sent.at[2 + which], recv_c.at[which, my_z], (my_row, c)
-        )
+            ref.at[my_col],
+            ref.at[my_col],
+            sent.at[2 + which],
+            recv_c.at[2 * across + which, my_z],
+            peer,
+        )
+
+    def send_line(z, first=0):
+        for which in (0, 1):
+            for m, peer in list(enumerate(line(z)))[first:]:
+                col_copy(peer, which, m > 0 and first == 0).start()
+
+    def learn(d):
+        for sign, _ in sides:
+            z, other = my_z + sign * d, my_z - sign
+            inside = jnp.logical_and(z >= 0, z < n_z)
+
+            @pl.when(inside)
+            def _():
+                pl.semaphore_wait(ready.at[z], 1)
+
+            @pl.when(jnp.logical_and(inside, jnp.logical_and(other >= 0, other < n_z)))
+            def _():
+                pl.semaphore_signal(
+                    ready.at[z], inc=1, device_id=line(other)[0], device_id_type=MESH
+                )
+
+            @pl.when(inside)
+            def _():
+                send_line(z)
 
     def term_copy(k, which):
         src, dst = ((shares, incoming), (share_sums, incoming_sums))[which]
@@ -218,40 +257,49 @@
         fh, fm = split2(first)
         sh, sm = split2(first * scaled)
         group = stack_rows(col_count, split3(alpha))
-        left = jnp.concatenate([fh, sh, fm, sm, group] + [jnp.zeros_like(group)] * 3, 0)
+        left = jnp.concatenate([fh, sh, fm, sm, group], 0)
         return col_aug, left
 
-    waiting, begun, made = [], set(), {}
+    waiting, begun, made = [], set(), set()
     slots = values.shape[0]
+    half = col_count // 2
     count = 0
 
-    def add_up():
+    def high_sums():
+        k, place, slot = waiting[0]
+        return jnp.dot(lefts[place], values[slot, 0:col_count], preferred_element_type=F32)
+
+    def mid_sums(high):
         k, place, slot = waiting.pop(0)
-        left = lefts[place]
-        more = jnp.dot(
-            jnp.concatenate([left, left], 1), values[slot], preferred_element_type=F32
-        )
-        more = more[0:80]
-        if k in begun:
-            acc[k] += more
-        else:
-            acc[k] = more
+        left = jnp.concatenate([lefts[place, 0:32], lefts[place, 64:80]], 0)
+        mid = jnp.dot(left, values[slot, col_count : 2 * col_count], preferred_element_type=F32)
+        parts = (high[0:32] + mid[0:32], high[32:64], high[64:80] + mid[32:48])
+        for at, more in zip((0, 32, 64), parts):
+            here = slice(at, at + more.shape[0])
+            if k in begun:
+                acc[k, here] += more
+            else:
+                acc[k, here] = more
         begun.add(k)
+
+    def exponents_of(aug, k):
+        return lax.dot_general(aug, row_aug[k], (((0,), (0,)), ((), ())), preferred_element_type=F32)
 
     def contribute(pairs, last=False):
         nonlocal count
         pairs = list(pairs)
         while waiting:
-            add_up()
+            mid_sums(high_sums())
         augs, exponents = {}, {}
 
         def settle_values(now):
             nonlocal count
-            high, mid = split2(jnp.exp2(exponents.pop(now)))
             slot = count % slots
             count += 1
-            values[slot, 0:col_count] = high
-            values[slot, col_count : 2 * col_count] = mid
+            for at, exponent in zip((0, half), exponents.pop(now)):
+                high, mid = split2(jnp.exp2(exponent))
+                values[slot, at : at + half] = high
+                values[slot, col_count + at : col_count + at + half] = mid
             waiting.append((pairs[now][1], pairs[now][0], slot))
 
         for now, (place, k) in enumerate(pairs):
@@ -259,63 +307,90 @@
                 augs[place], left = operands(ordered[place])
                 if place not in made:
                     lefts[place] = left
-                    made[place] = True
-            exponents[now] = lax.dot_general(
-                augs[place], row_aug[k], (((0,), (0,)), ((), ())), preferred_element_type=F32
-            )
-            if len(waiting) >= LAG - 1:
-                add_up()
+                    made.add(place)
+            near = exponents_of(augs[place][:, 0:half], k)
+            high = high_sums() if waiting else None
+            exponents[now] = near, exponents_of(augs[place][:, half:], k)
+            if high is not None:
+                mid_sums(high)
             if now:
                 settle_values(now - 1)
         while waiting:
-            add_up()
+            mid_sums(high_sums())
         settle_values(len(pairs) - 1)
         while last and waiting:
-            add_up()
+            mid_sums(high_sums())
 
     prepare_rows(0)
 
     with scope("bar"):
-        pl.semaphore_wait(barrier, row_size + col_size - 2)
+        beside = sum(there.astype(jnp.int32) for _, there in sides)
+        pl.semaphore_wait(barrier, row_size - 1 + n_y - 1 + beside * n_y)
 
     with scope("send"):
+        @pl.when(jnp.logical_and(sides[0][1], sides[1][1]))
+        def _():
+            for sign in (1, -1):
+                pl.semaphore_signal(
+                    ready.at[my_z + sign],
+                    inc=1,
+                    device_id=line(my_z - sign)[0],
+                    device_id_type=MESH,
+                )
+
+        send_line(my_z, 1)
         for k in row_steps:
             row_copy(k, 0).start()
-        for c in col_peers:
-            col_copy(c, 0).start()
-            col_copy(c, 1).start()
+        for sign, there in sides:
+
+            @pl.when(there)
+            def _():
+                send_line(my_z + sign)
+
         for k in row_steps:
             row_copy(k, 1).start()
 
     with scope("c00"):
         contribute([(0, 0)], last=True)
 
+    if n_z > 2:
+        with scope("rdy2"):
+            learn(2)
     with scope("w01"):
         row_arrival(1).wait_recv()
     with scope("c01"):
         prepare_rows(1)
         contribute([(0, 1)], last=True)
 
-    def arrive(z, chunks):
+    def arrive(z, chunks, across=0):
         for which, ref in enumerate((cols, col_alpha)):
-            bytes_of(ref, chunks, sent.at[2 + which], recv_c.at[which, z]).wait_recv()
-
-    with scope("wrow"):
-        for k in range(CORES, row_size):
-            row_arrival(k).wait_recv()
-        if n_y > 1:
+            bytes_of(ref, chunks, sent.at[2 + which], recv_c.at[2 * across + which, z]).wait_recv()
+
+    with scope("rdy3"):
+        for d in range(3, n_z):
+            learn(d)
+
+    early = range(min(CORES, row_size))
+    late = range(CORES, row_size)
+    if n_y > 1:
+        with scope("wy"):
             arrive(my_z, n_y - 1)
-    with scope("crow"):
-        for k in range(CORES, row_size):
-            prepare_rows(k)
-        contribute(
-            [(0, k) for k in range(CORES, row_size)]
-            + [(m, k) for m in range(1, n_y) for k in range(row_size)]
-        )
+        with scope("cy"):
+            contribute([(m, k) for m in range(1, n_y) for k in early])
+    if row_size > CORES:
+        with scope("wrow"):
+            for k in late:
+                row_arrival(k).wait_recv()
+        with scope("crow"):
+            for k in late:
+                prepare_rows(k)
+            contribute([(m, k) for m in range(n_y) for k in late])
 
     for at in range(1, n_z):
         with scope("wz"):
-            arrive(order[at], n_y)
+            arrive(order[at], 1)
+            if n_y > 1:
+                arrive(order[at], n_y - 1, across=1)
         with scope("cz"):
             contribute(
                 [(at * n_y + m, k) for m in range(n_y) for k in range(row_size)],
@@ -419,7 +494,7 @@
             pltpu.VMEM((row_size, 112, row_count), BF16),
             pltpu.VMEM((row_size, 80, row_count), F32),
             pltpu.VMEM((LAG + 1, 2 * col_count, row_count), BF16),
-            pltpu.VMEM((col_size, 128, col_count), BF16),
+            pltpu.VMEM((col_size, 80, col_count), BF16),
             pltpu.VMEM((row_size, dims, row_count), F32),
             pltpu.VMEM((row_size, 1, row_count), F32),
             pltpu.VMEM((row_size, dims, row_count), F32),
@@ -427,10 +502,11 @@
             pltpu.VMEM((8, 128), F32),
             pltpu.VMEM((n_all, 1, 128), F32),
             dma((5,)),
+            pltpu.SemaphoreType.REGULAR((n_z,)),
             dma((7,)),
             dma((row_size,)),
             dma((1,)),
-            dma((2, n_z)),
+            dma((4, n_z)),
             dma((2,)),
             dma((1,)),
         ],

time: 20.9 us -> 20 us (0.957)
  Pallas kernels: 20 us -> 19.1 us
    pallas_call x1, Pallas kernels: 19.4 us -> 18.4 us  [on_device(): pl.pallas_call(functools.partial(kernel, row_size, col_size), out_shape=(...]
where the time goes in v3:
time: 20 us; the launch traced here: 19.7 us
  Pallas kernels  19.1 us (96%)
  between operations  0.64 us (3%)
    pallas_call x1, Pallas kernels, on_device(): pl.pallas_call(functools.partial(kernel, row_size, col_size), out_shape=(...  18.4 us
    pallas_call x1, Pallas kernels, on_device(): pl.pallas_call(settle, out_shape=[jax.ShapeDtypeStruct(x.shape, x.dtype)...  0.65 us

profile of v3, /device:TPU:0, one launch (start us, length us, event | category | flops | bytes accessed | tf_op | source)
XLA Modules:
  0.0 19.7 jit_solution(14226211392361856835)
XLA Ops:
  0.6 18.4 %shard_map.76 = (f32[16,512]{1,0:T(8,128)S(1)}, f32[1,512]{1,0:T(1,128)S(1)}, f32[1,16]{1,0:T(1,128)S(1)}) custom-call(f32[16,512]{1,0:T(8,128)} %xr_hbm.1, f32[1,512]{1,0:T(1,128)} %bitcast.5, f32[16,256]{1,0:T(8,128)} %xc_hbm.1, f32[1,256]{1,0:T(1,128)} %bitcast.6, f32[1,16]{1,0:T(1,128)} %bitcast.7), custom_call_target="tpu_custom_call" | custom-call | tf_op jit(solution)/shard_map/pallas_call | solution.py:479
  19.1 0.6 %shard_map.77 = (f32[16,512]{1,0:T(8,128)}, f32[1,512]{1,0:T(1,128)}, f32[1,16]{1,0:T(1,128)}) custom-call(f32[16,512]{1,0:T(8,128)S(1)} %get-tuple-element.9.terms_in, f32[1,512]{1,0:T(1,128)S(1)} %get-tuple-element.10.sums_in, f32[1,16]{1,0:T(1,128)S(1)} %get-tuple-element.11.grad_in), custom_call_target="tpu_custom_call" | custom-call | tf_op jit(solution)/shard_map/pallas_call | solution.py:523

commit v4 on v3

--- a/solution.py
+++ b/solution.py
@@ -133,11 +133,12 @@
         return [(my_row, z * n_y + (my_y + m) % n_y) for m in range(n_y)]
 
     barrier = pltpu.get_barrier_semaphore()
-    for sign, there in sides:
-
-        @pl.when(there)
-        def _():
-            for peer in reversed(line(my_z + sign)):
+    for m in range(n_y):
+        for sign, there in sides:
+
+            @pl.when(there)
+            def _():
+                peer = line(my_z + sign)[n_y - 1 - m]
                 pl.semaphore_signal(barrier, inc=1, device_id=peer, device_id_type=MESH)
 
     for peer in line(my_z)[1:]:
@@ -187,7 +188,7 @@
     def send_line(z, first=0):
         for which in (0, 1):
             for m, peer in list(enumerate(line(z)))[first:]:
-                col_copy(peer, which, m > 0 and first == 0).start()
+                col_copy(peer, which, int(m > 0 and not first)).start()
 
     def learn(d):
         for sign, _ in sides:
@@ -281,6 +282,25 @@
             else:
                 acc[k, here] = more
         begun.add(k)
+        left_over[k] -= 1
+        if not left_over[k]:
+            finish(k)
+
+    left_over = {k: col_size for k in range(row_size)}
+    folds = []
+
+    def finish(k):
+        total = acc[k]
+        row_scaled = rows[k] * inverse
+        first = total[0:16] + total[32:48]
+        second = total[16:32] + total[48:64]
+        weight = total[64:65] + total[65:66] + total[66:67]
+        share = (0.5 * row_alpha[k]) * (
+            row_scaled * row_scaled * weight - 2.0 * row_scaled * first + second
+        )
+        shares[k] = share
+        share_sums[k] = weight
+        folds.append(sum(share[:, at : at + 128] for at in range(0, row_count, 128)))
 
     def exponents_of(aug, k):
         return lax.dot_general(aug, row_aug[k], (((0,), (0,)), ((), ())), preferred_element_type=F32)
@@ -372,57 +392,53 @@
 
     early = range(min(CORES, row_size))
     late = range(CORES, row_size)
-    if n_y > 1:
-        with scope("wy"):
+    straight = [(at, 0) for at in range(1, n_z)]
+    across = [(at, m) for at in range(1, n_z) for m in range(1, n_y)]
+    mixed = [one for pair in zip(across, straight[1:]) for one in pair]
+    mixed += across[len(straight) - 1 :] if straight else []
+    blocks = [straight[:1]] if straight else []
+    blocks += [mixed[at : at + 2] for at in range(0, len(mixed), 2)]
+
+    same, other = range(CORES, row_size, CORES), range(CORES + 1, row_size, CORES)
+    beside_y = [(0, m) for m in range(1, n_y)]
+    with scope("wrow"):
+        for k in same:
+            row_arrival(k).wait_recv()
+        if n_y > 1:
             arrive(my_z, n_y - 1)
-        with scope("cy"):
-            contribute([(m, k) for m in range(1, n_y) for k in early])
-    if row_size > CORES:
-        with scope("wrow"):
-            for k in late:
-                row_arrival(k).wait_recv()
-        with scope("crow"):
-            for k in late:
-                prepare_rows(k)
-            contribute([(m, k) for m in range(n_y) for k in late])
-
-    for at in range(1, n_z):
+    with scope("crow"):
+        for k in same:
+            prepare_rows(k)
+        contribute(
+            [(0, k) for k in same] + [(m, k) for _, m in beside_y for k in (*early, *same)]
+        )
+    with scope("wrow2"):
+        for k in other:
+            row_arrival(k).wait_recv()
+        for k in other:
+            prepare_rows(k)
+    blocks = [[(0, 0)] + beside_y + sum(blocks[:1], [])] + blocks[1:]
+
+    arrived = set()
+    for block in blocks:
+        last = block is blocks[-1]
         with scope("wz"):
-            arrive(order[at], 1)
-            if n_y > 1:
-                arrive(order[at], n_y - 1, across=1)
-        with scope("cz"):
-            contribute(
-                [(at * n_y + m, k) for m in range(n_y) for k in range(row_size)],
-                last=at == n_z - 1,
-            )
-
-    with scope("fold"):
-        bytes_of(row_alpha, row_size - 1, sent.at[1], recv_ra.at[0]).wait_recv()
-        folded = None
-        for k in range(row_size):
-            total = acc[k]
-            row_scaled = rows[k] * inverse
-            first = total[0:16] + total[32:48]
-            second = total[16:32] + total[48:64]
-            weight = total[64:65] + total[65:66] + total[66:67]
-            share = (0.5 * row_alpha[k]) * (
-                row_scaled * row_scaled * weight - 2.0 * row_scaled * first + second
-            )
-            shares[k] = share
-            share_sums[k] = weight
-            for at in range(0, row_count, 128):
-                piece = share[:, at : at + 128]
-                folded = piece if folded is None else folded + piece
-        gathered = lax.dot_general(
-            jnp.ones((8, 128), F32),
-            folded,
-            (((1,), (1,)), ((), ())),
-            precision=lax.Precision.HIGHEST,
-            preferred_element_type=F32,
-        )
-        part[...] = jnp.zeros_like(part)
-        part[:, 0:dims] = gathered
+            for at, m in block:
+                if at and (at, m > 0) not in arrived:
+                    arrived.add((at, m > 0))
+                    arrive(order[at], n_y - 1 if m else 1, across=int(m > 0))
+            if last:
+                bytes_of(row_alpha, row_size - 1, sent.at[1], recv_ra.at[0]).wait_recv()
+        with scope("fold" if last else "cz"):
+            pairs = [
+                (at * n_y + m, k) for at, m in block for k in (range(row_size) if at else other)
+            ]
+            if last:
+                pairs.sort(key=lambda pair: pair[1])
+            contribute(pairs, last=last)
+            if last:
+                part[...] = jnp.zeros_like(part)
+                part[0:1, 0:dims] = jnp.sum(sum(folds).T, 0, keepdims=True)
 
     with scope("gst"):
         for place in range(n_all - 1):

time: 20 us -> 19.7 us (0.985)
  Pallas kernels: 19.1 us -> 18.8 us
    pallas_call x1, Pallas kernels: 18.4 us -> 18.1 us  [on_device(): pl.pallas_call(functools.partial(kernel, row_size, col_size), out_shape=(...]
where the time goes in v4:
time: 19.7 us; the launch traced here: 19.4 us
  Pallas kernels  18.8 us (95%)
  between operations  0.64 us (3%)
    pallas_call x1, Pallas kernels, on_device(): pl.pallas_call(functools.partial(kernel, row_size, col_size), out_shape=(...  18.1 us
    pallas_call x1, Pallas kernels, on_device(): pl.pallas_call(settle, out_shape=[jax.ShapeDtypeStruct(x.shape, x.dtype)...  0.65 us

profile of v4, /device:TPU:0, one launch (start us, length us, event | category | flops | bytes accessed | tf_op | source)
XLA Modules:
  0.0 19.4 jit_solution(8742436326025357416)
XLA Ops:
  0.6 18.1 %shard_map.76 = (f32[16,512]{1,0:T(8,128)S(1)}, f32[1,512]{1,0:T(1,128)S(1)}, f32[1,16]{1,0:T(1,128)S(1)}) custom-call(f32[16,512]{1,0:T(8,128)} %xr_hbm.1, f32[1,512]{1,0:T(1,128)} %bitcast.5, f32[16,256]{1,0:T(8,128)} %xc_hbm.1, f32[1,256]{1,0:T(1,128)} %bitcast.6, f32[1,16]{1,0:T(1,128)} %bitcast.7), custom_call_target="tpu_custom_call" | custom-call | tf_op jit(solution)/shard_map/pallas_call | solution.py:495
  18.8 0.6 %shard_map.77 = (f32[16,512]{1,0:T(8,128)}, f32[1,512]{1,0:T(1,128)}, f32[1,16]{1,0:T(1,128)}) custom-call(f32[16,512]{1,0:T(8,128)S(1)} %get-tuple-element.9.terms_in, f32[1,512]{1,0:T(1,128)S(1)} %get-tuple-element.10.sums_in, f32[1,16]{1,0:T(1,128)S(1)} %get-tuple-element.11.grad_in), custom_call_target="tpu_custom_call" | custom-call | tf_op jit(solution)/shard_map/pallas_call | solution.py:539

commit v5 on v4

--- a/solution.py
+++ b/solution.py
@@ -89,11 +89,11 @@
     incoming_sums,
     part,
     parts,
+    tally,
     local,
     ready,
     sent,
     recv_r,
-    recv_ra,
     recv_c,
     recv_t,
     recv_g,
@@ -164,24 +164,25 @@
         return remote(
             ref.at[0],
             ref.at[there],
-            sent.at[which],
-            recv_ra.at[0] if which else recv_r.at[there],
+            sent.at[0],
+            recv_r.at[there],
             row_peer(k),
         )
 
-    def bytes_of(ref, count, send, recv):
-        return remote(ref.at[pl.ds(0, count)], ref.at[pl.ds(0, count)], send, recv, row_peer(1))
+    def bytes_of(blocks, count, send, recv):
+        size = pl.ds(0, blocks * (dims + 1) * count // 128)
+        return remote(tally.at[size], tally.at[size], send, recv, row_peer(1))
 
     def row_arrival(k):
-        return remote(rows.at[0], rows.at[k], sent.at[0], recv_r.at[k], row_peer(k))
+        bytes_of(1, row_count, sent.at[0], recv_r.at[k]).wait_recv()
 
     def col_copy(peer, which, across):
         ref = (cols, col_alpha)[which]
         return remote(
             ref.at[my_col],
             ref.at[my_col],
-            sent.at[2 + which],
-            recv_c.at[2 * across + which, my_z],
+            sent.at[1],
+            recv_c.at[across, my_z],
             peer,
         )
 
@@ -213,7 +214,7 @@
         src, dst = ((shares, incoming), (share_sums, incoming_sums))[which]
         there = back(k)
         return remote(
-            src.at[k], dst.at[there], sent.at[4 + which], recv_t.at[which], row_peer(k)
+            src.at[k], dst.at[there], sent.at[2], recv_t.at[0], row_peer(k)
         )
 
     steps = far_first(row_size, col_size)
@@ -225,7 +226,7 @@
             (my_z + dz) % n_z * n_y + (my_y + dy) % n_y,
         )
         return remote(
-            part.at[pl.ds(0, 1)], parts.at[place], sent.at[6], recv_g.at[0], peer
+            part.at[pl.ds(0, 1)], parts.at[place], sent.at[3], recv_g.at[0], peer
         )
 
     with scope("load"):
@@ -361,14 +362,12 @@
         send_line(my_z, 1)
         for k in row_steps:
             row_copy(k, 0).start()
+            row_copy(k, 1).start()
         for sign, there in sides:
 
             @pl.when(there)
             def _():
                 send_line(my_z + sign)
-
-        for k in row_steps:
-            row_copy(k, 1).start()
 
     with scope("c00"):
         contribute([(0, 0)], last=True)
@@ -377,14 +376,13 @@
         with scope("rdy2"):
             learn(2)
     with scope("w01"):
-        row_arrival(1).wait_recv()
+        row_arrival(1)
     with scope("c01"):
         prepare_rows(1)
         contribute([(0, 1)], last=True)
 
     def arrive(z, chunks, across=0):
-        for which, ref in enumerate((cols, col_alpha)):
-            bytes_of(ref, chunks, sent.at[2 + which], recv_c.at[2 * across + which, z]).wait_recv()
+        bytes_of(chunks, col_count, sent.at[1], recv_c.at[across, z]).wait_recv()
 
     with scope("rdy3"):
         for d in range(3, n_z):
@@ -403,7 +401,7 @@
     beside_y = [(0, m) for m in range(1, n_y)]
     with scope("wrow"):
         for k in same:
-            row_arrival(k).wait_recv()
+            row_arrival(k)
         if n_y > 1:
             arrive(my_z, n_y - 1)
     with scope("crow"):
@@ -414,7 +412,7 @@
         )
     with scope("wrow2"):
         for k in other:
-            row_arrival(k).wait_recv()
+            row_arrival(k)
         for k in other:
             prepare_rows(k)
     blocks = [[(0, 0)] + beside_y + sum(blocks[:1], [])] + blocks[1:]
@@ -427,8 +425,6 @@
                 if at and (at, m > 0) not in arrived:
                     arrived.add((at, m > 0))
                     arrive(order[at], n_y - 1 if m else 1, across=int(m > 0))
-            if last:
-                bytes_of(row_alpha, row_size - 1, sent.at[1], recv_ra.at[0]).wait_recv()
         with scope("fold" if last else "cz"):
             pairs = [
                 (at * n_y + m, k) for at, m in block for k in (range(row_size) if at else other)
@@ -448,14 +444,11 @@
                 term_copy(k, which).start()
 
     with scope("drain"):
-        for which, ref in enumerate((rows, row_alpha)):
-            bytes_of(ref, row_size - 1, sent.at[which], recv_r.at[0]).wait_send()
-        for which, ref in enumerate((cols, col_alpha)):
-            bytes_of(ref, col_size - 1, sent.at[2 + which], recv_r.at[0]).wait_send()
+        bytes_of(row_size - 1, row_count, sent.at[0], recv_r.at[0]).wait_send()
+        bytes_of(col_size - 1, col_count, sent.at[1], recv_r.at[0]).wait_send()
 
     with scope("twait"):
-        for which, ref in enumerate((incoming, incoming_sums)):
-            bytes_of(ref, row_size - 1, sent.at[4 + which], recv_t.at[which]).wait_recv()
+        bytes_of(row_size - 1, row_count, sent.at[2], recv_t.at[0]).wait_recv()
     with scope("tsum"):
         terms, sums = shares[0], share_sums[0]
         for k in range(1, row_size):
@@ -465,11 +458,16 @@
         sums_ref[...] = sums
         parts[n_all - 1] = part[0:1]
     with scope("gwait"):
-        bytes_of(parts, n_all - 1, sent.at[6], recv_g.at[0]).wait()
+        remote(
+            parts.at[pl.ds(0, n_all - 1)],
+            parts.at[pl.ds(0, n_all - 1)],
+            sent.at[3],
+            recv_g.at[0],
+            row_peer(1),
+        ).wait()
     with scope("gsum"):
         grad_ref[...] = (jnp.sum(parts[...], 0) / (row_count * n_all))[:, 0:dims]
-        for which, ref in enumerate((shares, share_sums)):
-            bytes_of(ref, row_size - 1, sent.at[4 + which], recv_t.at[which]).wait_send()
+        bytes_of(row_size - 1, row_count, sent.at[2], recv_t.at[0]).wait_send()
 
 
 def settle(terms_in, sums_in, grad_in, terms_out, sums_out, grad_out, sems):
@@ -489,6 +487,7 @@
     col_count = x_cols.shape[1]
     _, _, n_z = layout(row_size, col_size)
     n_all = row_size * col_size
+    most = max(row_size * row_count, col_size * col_count)
     vmem = pl.BlockSpec(memory_space=pltpu.VMEM)
     anywhere = pl.BlockSpec(memory_space=pl.ANY)
     dma = pltpu.SemaphoreType.DMA
@@ -517,13 +516,13 @@
             pltpu.VMEM((row_size, 1, row_count), F32),
             pltpu.VMEM((8, 128), F32),
             pltpu.VMEM((n_all, 1, 128), F32),
+            pltpu.VMEM((most * (dims + 1) // 128, 1, 128), F32),
             dma((5,)),
             pltpu.SemaphoreType.REGULAR((n_z,)),
-            dma((7,)),
+            dma((4,)),
             dma((row_size,)),
+            dma((2, n_z)),
             dma((1,)),
-            dma((4, n_z)),
-            dma((2,)),
             dma((1,)),
         ],
         compiler_params=pltpu.CompilerParams(

time: 19.7 us -> 19.5 us (0.990)
  no operation moved by 1% of the time
where the time goes in v5:
time: 19.5 us; the launch traced here: 19.3 us
  Pallas kernels  18.7 us (96%)
  between operations  0.64 us (3%)
    pallas_call x1, Pallas kernels, on_device(): pl.pallas_call(functools.partial(kernel, row_size, col_size), out_shape=(...  18 us
    pallas_call x1, Pallas kernels, on_device(): pl.pallas_call(settle, out_shape=[jax.ShapeDtypeStruct(x.shape, x.dtype)...  0.65 us

profile of v5, /device:TPU:0, one launch (start us, length us, event | category | flops | bytes accessed | tf_op | source)
XLA Modules:
  0.0 19.3 jit_solution(6955658355518416504)
XLA Ops:
  0.6 18.0 %shard_map.76 = (f32[16,512]{1,0:T(8,128)S(1)}, f32[1,512]{1,0:T(1,128)S(1)}, f32[1,16]{1,0:T(1,128)S(1)}) custom-call(f32[16,512]{1,0:T(8,128)} %xr_hbm.1, f32[1,512]{1,0:T(1,128)} %bitcast.5, f32[16,256]{1,0:T(8,128)} %xc_hbm.1, f32[1,256]{1,0:T(1,128)} %bitcast.6, f32[1,16]{1,0:T(1,128)} %bitcast.7), custom_call_target="tpu_custom_call" | custom-call | tf_op jit(solution)/shard_map/pallas_call | solution.py:494
  18.6 0.6 %shard_map.77 = (f32[16,512]{1,0:T(8,128)}, f32[1,512]{1,0:T(1,128)}, f32[1,16]{1,0:T(1,128)}) custom-call(f32[16,512]{1,0:T(8,128)S(1)} %get-tuple-element.9.terms_in, f32[1,512]{1,0:T(1,128)S(1)} %get-tuple-element.10.sums_in, f32[1,16]{1,0:T(1,128)S(1)} %get-tuple-element.11.grad_in), custom_call_target="tpu_custom_call" | custom-call | tf_op jit(solution)/shard_map/pallas_call | solution.py:538
